TPU v7x, 32 devices: a whole 2x2x4 slice. The times are simulated.
32 devices in a mesh: shard: 2 (over core), ctx: 8 (over z, x), tp: 2 (over y).
Axes of the slice: x: 2, y: 2, z: 4, core: 2. Of those that a mesh axis runs over, the one named last changes fastest.
Arguments:
- tokens: bfloat16 [2, 4096, 1024], P('shard', ('ctx', 'tp')), may hold values from -6 to 6
- value_first: bfloat16 [2, 4096, 1024], P('shard', ('ctx', 'tp')), may hold values from -6 to 6
- teacher: bfloat16 [2, 4096, 1024], P('shard', ('ctx', 'tp')), may hold values from -13 to 13
- valid: int32 [2, 4096], P('shard', ('ctx', 'tp')), may hold values from 0 to 1, as said below
- blocks: int32 [2, 4096], P('shard'), may hold values from 0 to 31, never falling along the last dimension, each value on 1 to 256 neighbouring positions
- gain_attn: float32 [1024], replicated, may hold values from 0.1 to 1.9
- gain_ffn: float32 [1024], replicated, may hold values from 0.1 to 1.9
- w_query: bfloat16 [1024, 1024], P('shard', 'tp'), may hold values from -0.375 to 0.375
- w_key: bfloat16 [1024, 1024], P('shard', 'tp'), may hold values from -0.1875 to 0.1875
- w_value: bfloat16 [1024, 1024], P('shard', 'tp'), may hold values from -0.1875 to 0.1875
- w_out: bfloat16 [1024, 1024], P('tp', 'shard'), may hold values from -0.75 to 0.75
- w_gate: bfloat16 [1024, 2816], P('shard', 'tp'), may hold values from -0.1875 to 0.1875
- w_up: bfloat16 [1024, 2816], P('shard', 'tp'), may hold values from -0.1875 to 0.1875
- w_down: bfloat16 [2816, 1024], P('tp', 'shard'), may hold values from -0.109375 to 0.109375
Outputs:
- output: bfloat16 [2, 4096, 1024], P('shard', ('ctx', 'tp'))
- loss: float32 [], replicated
- tokens_grad: float32 [2, 4096, 1024], P('shard', ('ctx', 'tp'))
- value_first_grad: float32 [2, 4096, 1024], P('shard', ('ctx', 'tp'))
- gain_attn_grad: float32 [1024], replicated
- gain_ffn_grad: float32 [1024], replicated
- w_query_grad: float32 [1024, 1024], P('shard', 'tp')
- w_key_grad: float32 [1024, 1024], P('shard', 'tp')
- w_value_grad: float32 [1024, 1024], P('shard', 'tp')
- w_out_grad: float32 [1024, 1024], P('tp', 'shard')
- w_gate_grad: float32 [1024, 2816], P('shard', 'tp')
- w_up_grad: float32 [1024, 2816], P('shard', 'tp')
- w_down_grad: float32 [2816, 1024], P('tp', 'shard')
Inputs may be any that keep to these rules, and one draw needn't show every extreme that they name: `blocks`: block numbers count from 0 and never fall along a sequence; each block holds 1 to 256 tokens, one exactly 256. The first token of every sequence is valid.
All inputs are finite; a program needn't handle non-finite values.
Results may differ from a plain program's by a relative error of at most 0.019.
Values may be sent and summed in bfloat16 or wider, within the bound.
No kernel may reach another device: no remote copies, remote signals or barrier semaphores. Data moves between devices by JAX's collectives and lax.ppermute only.
A program may use at most 256 MiB of HBM per device.

v0:
```python
import jax
import jax.numpy as jnp
from jax import lax
from jax.sharding import PartitionSpec as P

HEAD_DIM = 64
epsilon = 1e-06


def rms_norm(values, gain):
    return values * lax.rsqrt(jnp.mean(values * values, axis=-1, keepdims=True) + epsilon) * gain


def product(left, right):
    return jnp.dot(left, right, preferred_element_type=jnp.float32)


def product_nt(left, right):
    return lax.dot_general(
        left, right, (((1,), (1,)), ((), ())), preferred_element_type=jnp.float32
    )


def product_tn(left, right):
    return lax.dot_general(
        left, right, (((0,), (0,)), ((), ())), preferred_element_type=jnp.float32
    )


def head_slice(values, head_index):
    return lax.dynamic_slice_in_dim(values, head_index * HEAD_DIM, HEAD_DIM, 1)


def block_layout(query_count):
    return (query_count, query_count // query_count)


def heads_to_columns(stacked):
    return jnp.transpose(stacked, (1, 0, 2)).reshape(
        stacked.shape[1], stacked.shape[0] * stacked.shape[2]
    )


def attend_forward(queries, keys_all, values_all, query_marks, key_marks):
    query_count = queries.shape[0]
    block_size, block_count = block_layout(query_count)
    score_scale = HEAD_DIM ** (-0.5)

    def one_head(head_index):
        query_head = head_slice(queries, head_index)
        key_head = head_slice(keys_all, head_index)
        value_head = head_slice(values_all, head_index)

        def one_block(block_index):
            scores = product_nt(query_head, key_head) * score_scale
            scores = jnp.where(key_marks[None, :] <= query_marks[:, None], scores, -1e30)
            highest = jnp.max(scores, axis=1, keepdims=True)
            exponent = jnp.exp(scores - highest)
            totals = jnp.sum(exponent, axis=1, keepdims=True)
            weights = (exponent / totals).astype(jnp.bfloat16)
            return (product(weights, value_head), (highest + jnp.log(totals))[:, 0])

        outputs, log_totals = lax.map(one_block, jnp.arange(block_count))
        return (outputs.reshape(query_count, HEAD_DIM), log_totals.reshape(query_count))

    outputs, log_totals = lax.map(one_head, jnp.arange(queries.shape[1] // HEAD_DIM))
    return (heads_to_columns(outputs), log_totals)


def attend_backward(
    queries, keys_all, values_all, grad_attended, log_totals, query_marks, key_marks
):
    query_count = queries.shape[0]
    block_size, block_count = block_layout(query_count)
    score_scale = HEAD_DIM ** (-0.5)

    def one_head(item):
        head_index, head_totals = item
        query_head = head_slice(queries, head_index)
        key_head = head_slice(keys_all, head_index)
        value_head = head_slice(values_all, head_index)
        grad_head = head_slice(grad_attended, head_index)

        def one_block(carry, block_index):
            scores = product_nt(query_head, key_head) * score_scale
            scores = jnp.where(key_marks[None, :] <= query_marks[:, None], scores, -1e30)
            probs = jnp.exp(scores - head_totals[:, None])
            grad_probs = product_nt(grad_head, value_head)
            inner = jnp.sum(probs * grad_probs, axis=1, keepdims=True)
            grad_scores = (probs * (grad_probs - inner)).astype(jnp.bfloat16)
            query_grad = product(grad_scores, key_head) * score_scale
            key_grad, value_grad = carry
            key_grad = key_grad + product_tn(grad_scores, query_head) * score_scale
            value_grad = value_grad + product_tn(probs.astype(jnp.bfloat16), grad_head)
            return ((key_grad, value_grad), (query_grad, inner[:, 0]))

        empty = jnp.zeros((keys_all.shape[0], HEAD_DIM), jnp.float32)
        start_carry = (empty, empty)
        sums, outs = lax.scan(one_block, start_carry, jnp.arange(block_count))
        query_grad = outs[0].reshape(query_count, HEAD_DIM)
        return (query_grad, sums[0], sums[1])

    head_count = queries.shape[1] // HEAD_DIM
    results = lax.map(one_head, (jnp.arange(head_count), log_totals))
    return (
        heads_to_columns(results[0]),
        heads_to_columns(results[1]),
        heads_to_columns(results[2]),
    )


def on_device(
    tokens,
    value_first,
    teacher,
    valid,
    blocks,
    gain_attn,
    gain_ffn,
    w_query,
    w_key,
    w_value,
    w_out,
    w_gate,
    w_up,
    w_down,
):
    width = tokens.shape[2]
    own_rows = tokens.shape[1]
    group_rows = own_rows * lax.axis_size("tp")
    inputs = tokens.reshape(own_rows, width).astype(jnp.float32)
    key_marks = blocks.reshape(-1)
    query_marks = lax.dynamic_slice_in_dim(
        key_marks, lax.axis_index("ctx") * group_rows, group_rows, 0
    )
    gathered = (
        lax.all_gather(w_query, "shard", axis=0, tiled=True),
        lax.all_gather(w_key, "shard", axis=0, tiled=True),
        lax.all_gather(w_value, "shard", axis=0, tiled=True),
        lax.all_gather(w_gate, "shard", axis=0, tiled=True),
        lax.all_gather(w_up, "shard", axis=0, tiled=True),
        lax.all_gather(w_out, "shard", axis=1, tiled=True),
        lax.all_gather(w_down, "shard", axis=1, tiled=True),
    )
    weight_query, weight_key, weight_value, weight_gate, weight_up, weight_out, weight_down = (
        gathered
    )

    def spread(values):
        return lax.all_gather(values, "tp", axis=0, tiled=True)

    def collect(terms):
        return lax.psum_scatter(terms, "tp", scatter_dimension=0, tiled=True)

    normed_one = spread(rms_norm(inputs, gain_attn).astype(jnp.bfloat16))
    first_mine = lax.all_to_all(
        value_first.reshape(own_rows, width), "tp", split_axis=1, concat_axis=0, tiled=True
    )
    queries = product(normed_one, weight_query).astype(jnp.bfloat16)
    keys = product(normed_one, weight_key).astype(jnp.bfloat16)
    mixed = (0.5 * product(normed_one, weight_value) + 0.5 * first_mine.astype(jnp.float32)).astype(
        jnp.bfloat16
    )
    keys_all, mixed_all = (
        lax.all_gather(keys, "ctx", axis=0, tiled=True),
        lax.all_gather(mixed, "ctx", axis=0, tiled=True),
    )
    attended, log_totals = attend_forward(queries, keys_all, mixed_all, query_marks, key_marks)
    attended = attended.astype(jnp.bfloat16)
    hidden = inputs + collect(product(attended, weight_out))
    normed_two = spread(rms_norm(hidden, gain_ffn).astype(jnp.bfloat16))
    gate_value = product(normed_two, weight_gate)
    up_value = product(normed_two, weight_up)
    logistic = jax.nn.sigmoid(gate_value)
    activated = (gate_value * logistic * up_value).astype(jnp.bfloat16)
    final = hidden + collect(product(activated, weight_down))
    target = teacher.reshape(own_rows, width).astype(jnp.float32)
    keep = valid.reshape(own_rows).astype(jnp.float32)
    difference = final - target
    local_error = jnp.sum(jnp.mean(difference * difference, axis=1) * keep)
    error_sum, valid_count = lax.psum((local_error, jnp.sum(keep)), ("shard", "ctx", "tp"))
    loss = error_sum / valid_count
    token_total = group_rows * lax.axis_size("ctx") * lax.axis_size("shard")
    grad_final = token_total / valid_count * keep[:, None] * difference
    grad_round = spread(grad_final.astype(jnp.bfloat16))
    grad_act = product_nt(grad_round, weight_down)
    grad_gate = (grad_act * up_value * logistic * (1.0 + gate_value * (1.0 - logistic))).astype(
        jnp.bfloat16
    )
    grad_up = (grad_act * gate_value * logistic).astype(jnp.bfloat16)
    grad_two = collect(product_nt(grad_gate, weight_gate) + product_nt(grad_up, weight_up))
    norm_two_back = jax.vjp(rms_norm, hidden, gain_ffn)[1]
    hidden_part, gain_ffn_term = norm_two_back(grad_two)
    grad_hidden = grad_final + hidden_part
    hidden_round = spread(grad_hidden.astype(jnp.bfloat16))
    grad_attended = product_nt(hidden_round, weight_out).astype(jnp.bfloat16)
    query_grad, key_term, value_term = attend_backward(
        queries, keys_all, mixed_all, grad_attended, log_totals, query_marks, key_marks
    )
    key_sum, value_sum = (
        lax.psum_scatter(
            key_term.astype(jnp.bfloat16), "ctx", scatter_dimension=0, tiled=True
        ).astype(jnp.float32),
        lax.psum_scatter(
            value_term.astype(jnp.bfloat16), "ctx", scatter_dimension=0, tiled=True
        ).astype(jnp.float32),
    )
    query_round = query_grad.astype(jnp.bfloat16)
    key_round = key_sum.astype(jnp.bfloat16)
    value_half = (0.5 * value_sum).astype(jnp.bfloat16)
    grad_one = collect(
        product_nt(query_round, weight_query)
        + product_nt(key_round, weight_key)
        + product_nt(value_half, weight_value)
    )
    norm_one_back = jax.vjp(rms_norm, inputs, gain_attn)[1]
    input_part, gain_attn_term = norm_one_back(grad_one)
    tokens_grad = grad_hidden + input_part
    first_grad = lax.all_to_all(value_half, "tp", split_axis=0, concat_axis=1, tiled=True).astype(
        jnp.float32
    )
    gain_attn_grad, gain_ffn_grad = lax.psum(
        (gain_attn_term, gain_ffn_term), ("shard", "ctx", "tp")
    )
    piece = lax.psum_scatter(
        jnp.concatenate(
            [
                product_tn(normed_one, query_round),
                product_tn(normed_one, key_round),
                product_tn(normed_one, value_half),
                product_tn(hidden_round, attended),
                product_tn(normed_two, grad_gate),
                product_tn(normed_two, grad_up),
                product_tn(grad_round, activated),
            ],
            axis=1,
        ).astype(jnp.bfloat16),
        "shard",
        scatter_dimension=0,
        tiled=True,
    )
    summed = lax.psum(piece, "ctx").astype(jnp.float32)
    half_width = w_query.shape[1]
    hidden_width = w_gate.shape[1]
    offset_gate = 4 * half_width
    offset_up = offset_gate + hidden_width
    offset_down = offset_up + hidden_width
    w_query_grad = summed[:, 0:half_width]
    w_key_grad = summed[:, half_width : 2 * half_width]
    w_value_grad = summed[:, 2 * half_width : 3 * half_width]
    w_out_grad = jnp.transpose(summed[:, 3 * half_width : offset_gate])
    w_gate_grad = summed[:, offset_gate:offset_up]
    w_up_grad = summed[:, offset_up:offset_down]
    w_down_grad = jnp.transpose(summed[:, offset_down : offset_down + hidden_width])
    output = final.astype(jnp.bfloat16).reshape(1, own_rows, width)
    return (
        output,
        loss,
        tokens_grad.reshape(1, own_rows, width),
        first_grad.reshape(1, own_rows, width),
        gain_attn_grad,
        gain_ffn_grad,
        w_query_grad,
        w_key_grad,
        w_value_grad,
        w_out_grad,
        w_gate_grad,
        w_up_grad,
        w_down_grad,
    )


def solution(mesh):
    placed = (
        P("shard", ("ctx", "tp"), None),
        P("shard", ("ctx", "tp"), None),
        P("shard", ("ctx", "tp"), None),
        P("shard", ("ctx", "tp")),
        P("shard", None),
        P(),
        P(),
        P("shard", "tp"),
        P("shard", "tp"),
        P("shard", "tp"),
        P("tp", "shard"),
        P("shard", "tp"),
        P("shard", "tp"),
        P("tp", "shard"),
    )
    return jax.shard_map(
        on_device,
        mesh=mesh,
        in_specs=placed,
        out_specs=(
            P("shard", ("ctx", "tp"), None),
            P(),
            P("shard", ("ctx", "tp"), None),
            P("shard", ("ctx", "tp"), None),
            P(),
            P(),
            P("shard", "tp"),
            P("shard", "tp"),
            P("shard", "tp"),
            P("tp", "shard"),
            P("shard", "tp"),
            P("shard", "tp"),
            P("tp", "shard"),
        ),
        check_vma=False,
    )
```

profile of v0, /device:TPU:0, one launch (start us, length us, event | category | flops | bytes accessed | tf_op | source)
XLA Modules:
  0.0 1274.1 jit_solution(9744088578391808102)
XLA Ops:
  21.3 24.6 %all-gather.14.cloned.1.call-done = bf16[512,1024]{1,0:T(8,128)(2,1)} async-done(((bf16[256,1024]{1,0:T(8,128)(2,1)}), bf16[512,1024]{1,0:T(8,128)(2,1)}) %all-gather.14.cloned.1.call-update) | async-done | bytes 1048592 | tf_op jit(solution)/shard_map/all_gather | solution.py:150
  49.5 10.7 all_to_all.26
  70.1 75.2 %all-gather.20.cloned.1.call-done = bf16[4096,512]{1,0:T(8,128)(2,1)} async-done(((bf16[512,512]{1,0:T(8,128)(2,1)}), bf16[4096,512]{1,0:T(8,128)(2,1)}) %all-gather.20.cloned.1.call-update) | async-done | bytes 4194320 | tf_op jit(solution)/shard_map/all_gather | solution.py:165
  145.3 74.2 %all-gather.24.cloned.1.call-done = bf16[4096,512]{1,0:T(8,128)(2,1)} async-done(((bf16[512,512]{1,0:T(8,128)(2,1)}), bf16[4096,512]{1,0:T(8,128)(2,1)}) %all-gather.24.cloned.1.call-update) | async-done | bytes 4194320 | tf_op jit(solution)/shard_map/all_gather | solution.py:166
  219.6 73.0 %while.10 = (s32[]{:T(128)}, bf16[8,512,64]{1,2,0:T(8,128)(2,1)S(1)}, f32[8,512]{1,0:T(8,128)S(1)}, s32[1,4096]{1,0:T(1,128)S(1)}, s32[512]{0:T(512)S(1)}, /*ind...) while((s32[]{:T(128)}, ...), condition=%wide.region_4.0_spmd, body=%wide.region_1.4_spmd.sunk | while | flops 555744768 | bytes 27565260 | solution.py:66
  297.0 29.4 %reduce-scatter.8.cloned.1.call-done = f32[256,1024]{1,0:T(8,128)} async-done(((f32[512,1024]{1,0:T(8,128)}), f32[256,1024]{1,0:T(8,128)}) %reduce-scatter.8.cloned.1.call-update) | async-done | bytes 1048592 | tf_op jit(solution)/shard_map/reduce_scatter | solution.py:153
  330.4 9.4 all-gather.30.cloned.1.call-done
  339.8 24.6 %all-gather.28.cloned.1.call-done = bf16[512,1024]{1,0:T(8,128)(2,1)} async-done(((bf16[256,1024]{1,0:T(8,128)(2,1)}), bf16[512,1024]{1,0:T(8,128)(2,1)}) %all-gather.28.cloned.1.call-update) | async-done | bytes 1048592 | tf_op jit(solution)/shard_map/all_gather | solution.py:150
  398.3 40.9 %psum.36 = f32[]{:T(128)} all-reduce(f32[]{:T(128)} %convert_reduce_fusion), channel_id=1, replica_groups=mesh['shard'=2,'ctx'=8,'tp'=2] {'shard','ctx','tp'}, use_global_device_ids=true, to_apply=%region_12.13 | all-reduce | flops 1 | bytes 8 | tf_op jit(solution)/shard_map/psum | solution.py:181
  442.2 21.4 %all-gather.36.cloned.1.call-done = bf16[512,1024]{1,0:T(8,128)(2,1)} async-done(((bf16[256,1024]{1,0:T(8,128)(2,1)}), bf16[512,1024]{1,0:T(8,128)(2,1)}) %all-gather.36.cloned.1.call-update) | async-done | bytes 1048592 | tf_op jit(solution)/shard_map/all_gather | solution.py:150
  476.2 31.9 %reduce-scatter.12.cloned.1.call-done = f32[256,1024]{1,0:T(8,128)} async-done(((f32[512,1024]{1,0:T(8,128)}), f32[256,1024]{1,0:T(8,128)}) %reduce-scatter.12.cloned.1.call-update) | async-done | bytes 1048592 | tf_op jit(solution)/shard_map/reduce_scatter | solution.py:153
  512.6 21.2 %all-gather.38.cloned.1.call-done = bf16[512,1024]{1,0:T(8,128)(2,1)} async-done(((bf16[256,1024]{1,0:T(8,128)(2,1)}), bf16[512,1024]{1,0:T(8,128)(2,1)}) %all-gather.38.cloned.1.call-update) | async-done | bytes 1048592 | tf_op jit(solution)/shard_map/all_gather | solution.py:150
  536.1 233.1 %while.27 = (s32[]{:T(128)}, bf16[8,512,64]{1,2,0:T(8,128)(2,1)S(1)}, bf16[8,4096,64]{1,2,0:T(8,128)(2,1)}, bf16[8,4096,64]{1,2,0:T(8,128)(2,1)}, s32[1,4096]{1,...) while((s32[]{:T(128)}, ...), condition=%wide.region_17.18_spmd, body=%wide.region_15.17_spmd.sunk | while | flops 1363443200 | bytes 102398224 | solution.py:104
  547.4 7.9 multiply_convert_fusion.10
  576.5 7.9 multiply_convert_fusion.10
  605.6 7.9 multiply_convert_fusion.10
  634.8 7.9 multiply_convert_fusion.10
  783.2 74.6 %reduce-scatter.14.cloned.1.call-done = bf16[512,512]{0,1:T(8,128)(2,1)} async-done(((bf16[4096,512]{0,1:T(8,128)(2,1)}), bf16[512,512]{0,1:T(8,128)(2,1)}) %reduce-scatter.14.cloned.1.call-update) | async-done | bytes 524304 | tf_op jit(solution)/shard_map/reduce_scatter | solution.py:201
  860.5 88.7 %reduce-scatter.16.cloned.1.call-done = bf16[512,512]{1,0:T(8,128)(2,1)} async-done(((bf16[4096,512]{1,0:T(8,128)(2,1)}), bf16[512,512]{1,0:T(8,128)(2,1)}) %reduce-scatter.16.cloned.1.call-update) | async-done | bytes 524304 | tf_op jit(solution)/shard_map/reduce_scatter | solution.py:204
  973.8 15.7 %reduce-scatter.20.cloned.1.call-done = bf16[512,6272]{1,0:T(8,128)(2,1)} async-done(((bf16[1024,6272]{1,0:T(8,128)(2,1)}), bf16[512,6272]{1,0:T(8,128)(2,1)}) %reduce-scatter.20.cloned.1.call-update) | async-done | bytes 6422544 | tf_op jit(solution)/shard_map/reduce_scatter | solution.py:225
  994.7 10.0 all-to-all-done.1
  1007.4 19.2 %reduce-scatter.18.cloned.1.call-done = f32[256,1024]{1,0:T(8,128)} async-done(((f32[512,1024]{1,0:T(8,128)}), f32[256,1024]{1,0:T(8,128)}) %reduce-scatter.18.cloned.1.call-update) | async-done | bytes 1048592 | tf_op jit(solution)/shard_map/reduce_scatter | solution.py:153
  1028.2 43.5 %all-reduce = (f32[]{:T(128)}, f32[1024]{0:T(1024)}, f32[1024]{0:T(1024)}) all-reduce(f32[]{:T(128)} %multiply_reduce_fusion.5, f32[1024]{0:T(1024)S(1)} %get-tuple-element.215, f32[1024]{0:T(1024)S(1)} %copy-done.19), channel_id=1, replica_groups=mesh['shard'=2,'ctx'=8,'tp'=2] {'shard','ctx','tp'}, use_global_device_ids=true, to_apply=%region_10.11 | all-reduce | flops 2049 | bytes 16392 | tf_op jit(solution)/shard_map/psum | solution.py:181
  1075.7 172.6 %all-reduce.3.cloned.1.call-done = bf16[512,6272]{1,0:T(8,128)(2,1)} async-done(((bf16[512,6272]{1,0:T(8,128)(2,1)}), bf16[512,6272]{1,0:T(8,128)(2,1)}) %all-reduce.3.cloned.1.call-update) | async-done | bytes 6422544 | tf_op jit(solution)/shard_map/psum | solution.py:242
  (317 shorter events, 425.3 us)
Async XLA Ops:
  7.2 14.1 %all-gather.18.cloned.1.call-start = ((), (), s32[]{:S(2)}) async-start(), calls=%async_computation.11 | async-start | bytes 1572864 | tf_op jit(solution)/shard_map/all_gather | solution.py:138
  7.9 38.0 %all-gather.14.cloned.1.call-start = ((), (), s32[]{:S(2)}) async-start(), calls=%async_computation.9 | async-start | bytes 1572864 | tf_op jit(solution)/shard_map/all_gather | solution.py:150
  12.4 48.0 %all-gather.22.cloned.1.call-start = ((), (), s32[]{:S(2)}) async-start(), calls=%async_computation.13 | async-start | bytes 1572864 | tf_op jit(solution)/shard_map/all_gather | solution.py:139
  13.1 55.1 %all-gather.16.cloned.1.call-start = ((), (), s32[]{:S(2)}) async-start(), calls=%async_computation.10 | async-start | bytes 1572864 | tf_op jit(solution)/shard_map/all_gather | solution.py:137
  13.7 131.6 %all-gather.20.cloned.1.call-start = ((), (), s32[]{:S(2)}) async-start(), calls=%async_computation.12 | async-start | bytes 4718592 | tf_op jit(solution)/shard_map/all_gather | solution.py:165
  49.0 170.6 %all-gather.24.cloned.1.call-start = ((), (), s32[]{:S(2)}) async-start(), calls=%async_computation.14 | async-start | bytes 4718592 | tf_op jit(solution)/shard_map/all_gather | solution.py:166
  63.1 229.6 %all-gather.26.cloned.1.call-start = ((), (), s32[]{:S(2)}) async-start(), calls=%async_computation.15 | async-start | bytes 1572864 | tf_op jit(solution)/shard_map/all_gather | solution.py:142
  63.9 262.6 %reduce-scatter.8.cloned.1.call-start = ((), (), s32[]{:S(2)}) async-start(), calls=%async_computation.16 | async-start | bytes 3145728 | tf_op jit(solution)/shard_map/reduce_scatter | solution.py:153
  296.2 43.6 %all-gather.30.cloned.1.call-start = ((), (), s32[]{:S(2)}) async-start(), calls=%async_computation.18 | async-start | bytes 4325376 | tf_op jit(solution)/shard_map/all_gather | solution.py:140
  297.0 67.4 %all-gather.28.cloned.1.call-start = ((), (), s32[]{:S(2)}) async-start(), calls=%async_computation.17 | async-start | bytes 1572864 | tf_op jit(solution)/shard_map/all_gather | solution.py:150
  328.9 48.9 %all-gather.32.cloned.1.call-start = ((), (), s32[]{:S(2)}) async-start(), calls=%async_computation.19 | async-start | bytes 4325376 | tf_op jit(solution)/shard_map/all_gather | solution.py:141
  329.6 62.6 %all-gather.34.cloned.1.call-start = ((), (), s32[]{:S(2)}) async-start(), calls=%async_computation.20 | async-start | bytes 4325376 | tf_op jit(solution)/shard_map/all_gather | solution.py:143
  330.2 109.7 %reduce-scatter.10.cloned.1.call-start = ((), (), s32[]{:S(2)}) async-start(), calls=%async_computation.21 | async-start | bytes 3145728 | tf_op jit(solution)/shard_map/reduce_scatter | solution.py:153
  397.6 66.0 %all-gather.36.cloned.1.call-start = ((), (), s32[]{:S(2)}) async-start(), calls=%async_computation.22 | async-start | bytes 1572864 | tf_op jit(solution)/shard_map/all_gather | solution.py:150
  442.1 66.0 %reduce-scatter.12.cloned.1.call-start = ((), (), s32[]{:S(2)}) async-start(), calls=%async_computation.23 | async-start | bytes 3145728 | tf_op jit(solution)/shard_map/reduce_scatter | solution.py:153
  476.2 57.6 %all-gather.38.cloned.1.call-start = ((), (), s32[]{:S(2)}) async-start(), calls=%async_computation.24 | async-start | bytes 1572864 | tf_op jit(solution)/shard_map/all_gather | solution.py:150
  512.3 345.5 %reduce-scatter.14.cloned.1.call-start = ((), (), s32[]{:S(2)}) async-start(), calls=%async_computation.25 | async-start | bytes 4718592 | tf_op jit(solution)/shard_map/reduce_scatter | solution.py:201
  769.2 180.0 %reduce-scatter.16.cloned.1.call-start = ((), (), s32[]{:S(2)}) async-start(), calls=%async_computation.26 | async-start | bytes 4718592 | tf_op jit(solution)/shard_map/reduce_scatter | solution.py:204
  775.9 213.6 %reduce-scatter.20.cloned.1.call-start = ((), (), s32[]{:S(2)}) async-start(), calls=%async_computation.28 | async-start | bytes 19267584 | tf_op jit(solution)/shard_map/reduce_scatter | solution.py:225
  967.8 58.8 %reduce-scatter.18.cloned.1.call-start = ((), (), s32[]{:S(2)}) async-start(), calls=%async_computation.27 | async-start | bytes 3145728 | tf_op jit(solution)/shard_map/reduce_scatter | solution.py:153
  973.7 274.6 %all-reduce.3.cloned.1.call-start = ((), (), s32[]{:S(2)}) async-start(), calls=%async_computation.29 | async-start | bytes 12845056 | tf_op jit(solution)/shard_map/psum | solution.py:242
  990.4 14.2 %all-to-all-start.1 = ((bf16[2,256,512]{2,1,0:T(8,128)(2,1)}), bf16[2,256,512]{2,1,0:T(8,128)(2,1)S(1)}, u32[]{:S(2)}, u32[]{:S(2)}) async-start(bf16[2,256,512]{2,1,0:T(8,128)(2,1)} %bitcast.27), calls=%async_computation.7 | async-start | bytes 1048576 | tf_op jit(solution)/shard_map/all_to_all | solution.py:219
  1004.7 68.3 %copy-start.23 = (f32[256]{0:T(256)S(1)}, f32[256]{0:T(256)}, u32[]{:S(2)}) copy-start(f32[256]{0:T(256)} %copy-done.22) | copy-start | bytes 3076
  1004.7 68.3 %copy-start.5 = (f32[256,1024]{1,0:T(8,128)S(1)}, f32[256,1024]{1,0:T(8,128)}, u32[]{:S(2)}) copy-start(f32[256,1024]{1,0:T(8,128)} %get-tuple-element.264) | copy-start | bytes 3145732
  (43 other events, 496.3 us)
Sparse Core Ops, SparseCore 0:
  9.6 11.7 all-gather.17
  23.4 22.4 all-gather.13
  47.5 9.0 all-gather.21
  58.0 10.1 all-gather.15
  70.8 74.5 all-gather.19
  147.9 71.6 all-gather.23
  221.1 7.2 all-gather.25
  296.3 30.0 reduce-scatter.7
  328.0 11.7 all-gather.29
  341.8 22.4 all-gather.27
  366.0 11.7 all-gather.31
  379.2 12.8 all-gather.33
  397.7 33.4 reduce-scatter.9
  442.3 21.2 all-gather.35
  476.3 31.8 reduce-scatter.11
  512.4 21.2 all-gather.37
  769.3 88.4 reduce-scatter.13
  861.3 87.7 reduce-scatter.15
  967.9 21.5 reduce-scatter.19
  992.2 34.3 reduce-scatter.17
  1030.4 217.8 all-reduce.2
where the time goes:
time: 1280 us; the launch traced here: 1270 us
  waiting for transfers between devices  725 us (57%)
  matrix products  278 us (22%)
  other arithmetic  95.9 us (7%)
  blocking collectives  95.1 us (7%)
  local copies, waits for them, and re-layouts  45.2 us (4%)
  between operations  18.3 us (1%)
    psum x1, waiting for transfers between devices, on_device(): summed = lax.psum(piece, 'ctx').astype(jnp.float32)  173 us
    dot_general x31, matrix products, product_nt(): lax.dot_general(left, right, (((1,), (1,)), ((), ())), preferred_element_...  123 us
    all_gather x4, waiting for transfers between devices, spread(): return lax.all_gather(values, 'tp', axis=0, tiled=True)  91.8 us
    reduce_scatter x1, waiting for transfers between devices, on_device(): lax.psum_scatter(value_term.astype(jnp.bfloat16), 'ctx', scatter_dimensio...  88.7 us
    psum x2, blocking collectives, on_device(): lax.psum((local_error, jnp.sum(keep)), ('shard', 'ctx', 'tp'))  84.4 us
    reduce_scatter x4, waiting for transfers between devices, collect(): return lax.psum_scatter(terms, 'tp', scatter_dimension=0, tiled=True)  80.5 us
    dot_general x23, matrix products, product(): return jnp.dot(left, right, preferred_element_type=jnp.float32)  79.6 us
    dot_general x23, matrix products, product_tn(): lax.dot_general(left, right, (((0,), (0,)), ((), ())), preferred_element_...  75.3 us
  transfers between devices with their start and end apart: 22, of which 19 were waited for; matrix products, arithmetic and copies ran while one was open for 10% of the time, Pallas kernels for 0%

commit v1 on v0

--- a/solution.py
+++ b/solution.py
@@ -239,7 +239,7 @@
         scatter_dimension=0,
         tiled=True,
     )
-    summed = lax.psum(piece, "ctx").astype(jnp.float32)
+    summed = jnp.sum(lax.all_gather(piece, "ctx"), axis=0).astype(jnp.float32)
     half_width = w_query.shape[1]
     hidden_width = w_gate.shape[1]
     offset_gate = 4 * half_width

time: 1280 us -> 2040 us (1.59)
  waiting for transfers between devices: 725 us -> 1400 us
  blocking collectives: 95.1 us -> 174 us
  other arithmetic: 95.9 us -> 123 us
  matrix products: 278 us -> 253 us
    all_gather x0 -> x1, waiting for transfers between devices: none -> 848 us  [on_device(): summed = jnp.sum(lax.all_gather(piece, 'ctx'), axis=0).astype(jnp.float32)]
    psum x1 -> x0, waiting for transfers between devices: 173 us -> none  [on_device(): summed = lax.psum(piece, 'ctx').astype(jnp.float32)]
    psum x2, blocking collectives: 84.4 us -> 163 us  [on_device(): lax.psum((local_error, jnp.sum(keep)), ('shard', 'ctx', 'tp'))]
    dot_general x23, matrix products: 75.3 us -> 47.9 us  [product_tn(): lax.dot_general(left, right, (((0,), (0,)), ((), ())), preferred_element_...]
    reduce_sum x0 -> x1, other arithmetic: none -> 22 us  [on_device(): summed = jnp.sum(lax.all_gather(piece, 'ctx'), axis=0).astype(jnp.float32)]
  transfers between devices with their start and end apart: 22 -> 22, of which waited for: 19 -> 19; matrix products, arithmetic and copies ran while one was open for 10% -> 6% of each run, Pallas kernels for 0% -> 0%
where the time goes in v1:
time: 2040 us; the launch traced here: 2030 us
  waiting for transfers between devices  1400 us (69%)
  matrix products  253 us (12%)
  blocking collectives  174 us (9%)
  other arithmetic  123 us (6%)
  local copies, waits for them, and re-layouts  45.8 us (2%)
    all_gather x1, waiting for transfers between devices, on_device(): summed = jnp.sum(lax.all_gather(piece, 'ctx'), axis=0).astype(jnp.float32)  848 us
    psum x2, blocking collectives, on_device(): lax.psum((local_error, jnp.sum(keep)), ('shard', 'ctx', 'tp'))  163 us
    dot_general x31, matrix products, product_nt(): lax.dot_general(left, right, (((1,), (1,)), ((), ())), preferred_element_...  124 us
    all_gather x4, waiting for transfers between devices, spread(): return lax.all_gather(values, 'tp', axis=0, tiled=True)  89.2 us
    reduce_scatter x1, waiting for transfers between devices, on_device(): lax.psum_scatter(value_term.astype(jnp.bfloat16), 'ctx', scatter_dimensio...  88.7 us
    dot_general x23, matrix products, product(): return jnp.dot(left, right, preferred_element_type=jnp.float32)  80.9 us
    reduce_scatter x4, waiting for transfers between devices, collect(): return lax.psum_scatter(terms, 'tp', scatter_dimension=0, tiled=True)  80.4 us
    reduce_scatter x1, waiting for transfers between devices, on_device(): lax.psum_scatter(key_term.astype(jnp.bfloat16), 'ctx', scatter_dimension=...  75.3 us
  transfers between devices with their start and end apart: 22, of which 19 were waited for; matrix products, arithmetic and copies ran while one was open for 6% of the time, Pallas kernels for 0%

profile of v1, /device:TPU:0, one launch (start us, length us, event | category | flops | bytes accessed | tf_op | source)
XLA Modules:
  0.0 2031.4 jit_solution(12606343090748259480)
XLA Ops:
  13.8 22.1 %all-gather.16.cloned.1.call-done = bf16[512,1024]{1,0:T(8,128)(2,1)} async-done(((bf16[256,1024]{1,0:T(8,128)(2,1)}), bf16[512,1024]{1,0:T(8,128)(2,1)}) %all-gather.16.cloned.1.call-update) | async-done | bytes 1048592 | tf_op jit(solution)/shard_map/all_gather | solution.py:150
  35.9 10.6 all-gather.20.cloned.1.call-done
  50.1 11.2 all_to_all.26
  71.8 75.2 %all-gather.22.cloned.1.call-done = bf16[4096,512]{1,0:T(8,128)(2,1)} async-done(((bf16[512,512]{1,0:T(8,128)(2,1)}), bf16[4096,512]{1,0:T(8,128)(2,1)}) %all-gather.22.cloned.1.call-update) | async-done | bytes 4194320 | tf_op jit(solution)/shard_map/all_gather | solution.py:165
  147.1 74.2 %all-gather.26.cloned.1.call-done = bf16[4096,512]{1,0:T(8,128)(2,1)} async-done(((bf16[512,512]{1,0:T(8,128)(2,1)}), bf16[4096,512]{1,0:T(8,128)(2,1)}) %all-gather.26.cloned.1.call-update) | async-done | bytes 4194320 | tf_op jit(solution)/shard_map/all_gather | solution.py:166
  221.4 73.0 %while.10 = (s32[]{:T(128)}, bf16[8,512,64]{1,2,0:T(8,128)(2,1)S(1)}, f32[8,512]{1,0:T(8,128)S(1)}, s32[1,4096]{1,0:T(1,128)S(1)}, s32[512]{0:T(512)S(1)}, /*ind...) while((s32[]{:T(128)}, ...), condition=%wide.region_4.0_spmd, body=%wide.region_1.4_spmd.sunk | while | flops 555744768 | bytes 27565260 | solution.py:66
  298.7 29.4 %reduce-scatter.8.cloned.1.call-done = f32[256,1024]{1,0:T(8,128)} async-done(((f32[512,1024]{1,0:T(8,128)}), f32[256,1024]{1,0:T(8,128)}) %reduce-scatter.8.cloned.1.call-update) | async-done | bytes 1048592 | tf_op jit(solution)/shard_map/reduce_scatter | solution.py:153
  332.1 9.4 all-gather.32.cloned.1.call-done
  341.6 24.6 %all-gather.30.cloned.1.call-done = bf16[512,1024]{1,0:T(8,128)(2,1)} async-done(((bf16[256,1024]{1,0:T(8,128)(2,1)}), bf16[512,1024]{1,0:T(8,128)(2,1)}) %all-gather.30.cloned.1.call-update) | async-done | bytes 1048592 | tf_op jit(solution)/shard_map/all_gather | solution.py:150
  400.0 40.9 %psum.29 = f32[]{:T(128)} all-reduce(f32[]{:T(128)} %convert_reduce_fusion), channel_id=1, replica_groups=mesh['shard'=2,'ctx'=8,'tp'=2] {'shard','ctx','tp'}, use_global_device_ids=true, to_apply=%region_12.13 | all-reduce | flops 1 | bytes 8 | tf_op jit(solution)/shard_map/psum | solution.py:181
  443.9 21.4 %all-gather.38.cloned.1.call-done = bf16[512,1024]{1,0:T(8,128)(2,1)} async-done(((bf16[256,1024]{1,0:T(8,128)(2,1)}), bf16[512,1024]{1,0:T(8,128)(2,1)}) %all-gather.38.cloned.1.call-update) | async-done | bytes 1048592 | tf_op jit(solution)/shard_map/all_gather | solution.py:150
  477.9 31.9 %reduce-scatter.12.cloned.1.call-done = f32[256,1024]{1,0:T(8,128)} async-done(((f32[512,1024]{1,0:T(8,128)}), f32[256,1024]{1,0:T(8,128)}) %reduce-scatter.12.cloned.1.call-update) | async-done | bytes 1048592 | tf_op jit(solution)/shard_map/reduce_scatter | solution.py:153
  514.3 21.2 %all-gather.40.cloned.1.call-done = bf16[512,1024]{1,0:T(8,128)(2,1)} async-done(((bf16[256,1024]{1,0:T(8,128)(2,1)}), bf16[512,1024]{1,0:T(8,128)(2,1)}) %all-gather.40.cloned.1.call-update) | async-done | bytes 1048592 | tf_op jit(solution)/shard_map/all_gather | solution.py:150
  537.9 207.3 %while.27 = (s32[]{:T(128)}, bf16[8,512,64]{1,2,0:T(8,128)(2,1)S(1)}, bf16[8,4096,64]{1,2,0:T(8,128)(2,1)}, bf16[8,4096,64]{1,2,0:T(8,128)(2,1)}, s32[1,4096]{1,...) while((s32[]{:T(128)}, ...), condition=%wide.region_17.18_spmd, body=%wide.region_15.17_spmd.sunk | while | flops 1363443200 | bytes 135952688 | solution.py:104
  549.1 7.9 multiply_convert_fusion.10
  758.5 75.3 %reduce-scatter.14.cloned.1.call-done = bf16[512,512]{0,1:T(8,128)(2,1)} async-done(((bf16[4096,512]{0,1:T(8,128)(2,1)}), bf16[512,512]{0,1:T(8,128)(2,1)}) %reduce-scatter.14.cloned.1.call-update) | async-done | bytes 524304 | tf_op jit(solution)/shard_map/reduce_scatter | solution.py:201
  836.5 88.7 %reduce-scatter.16.cloned.1.call-done = bf16[512,512]{1,0:T(8,128)(2,1)} async-done(((bf16[4096,512]{1,0:T(8,128)(2,1)}), bf16[512,512]{1,0:T(8,128)(2,1)}) %reduce-scatter.16.cloned.1.call-update) | async-done | bytes 524304 | tf_op jit(solution)/shard_map/reduce_scatter | solution.py:204
  950.5 14.7 reduce-scatter.20.cloned.1.call-done
  970.5 10.1 all-to-all-done.1
  983.5 19.0 reduce-scatter.18.cloned.1.call-done
  1004.1 121.9 %all-reduce = (f32[]{:T(128)}, f32[1024]{0:T(1024)}, f32[1024]{0:T(1024)}) all-reduce(f32[]{:T(128)} %multiply_reduce_fusion.5, f32[1024]{0:T(1024)S(1)} %get-tuple-element.228, f32[1024]{0:T(1024)S(1)} %copy-done.19), channel_id=1, replica_groups=mesh['shard'=2,'ctx'=8,'tp'=2] {'shard','ctx','tp'}, use_global_device_ids=true, to_apply=%region_10.11 | all-reduce | flops 2049 | bytes 16392 | tf_op jit(solution)/shard_map/psum | solution.py:181
  1129.8 847.7 %all-gather.42.cloned.1.call-done = bf16[4096,6272]{1,0:T(8,128)(2,1)} async-done(((bf16[512,6272]{1,0:T(8,128)(2,1)}), bf16[4096,6272]{1,0:T(8,128)(2,1)}) %all-gather.42.cloned.1.call-update) | async-done | bytes 51380240 | tf_op jit(solution)/shard_map/all_gather | solution.py:242
  1977.5 22.0 %reduce_sum.146 = bf16[512,6272]{1,0:T(8,128)(2,1)} reduce(bf16[8,512,6272]{2,1,0:T(8,128)(2,1)} %bitcast.138, bf16[]{:T(256)} %constant.109.clone.1), dimensions={0}, to_apply=%region_27.28 | reduce | flops 22478848 | bytes 57802752 | tf_op jit(solution)/shard_map/reduce_sum | solution.py:242
  2002.8 8.5 convert_element_type.183
  (337 shorter events, 414.0 us)
Async XLA Ops:
  7.2 28.7 %all-gather.16.cloned.1.call-start = ((), (), s32[]{:S(2)}) async-start(), calls=%async_computation.9 | async-start | bytes 1572864 | tf_op jit(solution)/shard_map/all_gather | solution.py:150
  11.7 34.8 %all-gather.20.cloned.1.call-start = ((), (), s32[]{:S(2)}) async-start(), calls=%async_computation.11 | async-start | bytes 1572864 | tf_op jit(solution)/shard_map/all_gather | solution.py:138
  12.5 49.0 %all-gather.24.cloned.1.call-start = ((), (), s32[]{:S(2)}) async-start(), calls=%async_computation.13 | async-start | bytes 1572864 | tf_op jit(solution)/shard_map/all_gather | solution.py:139
  13.2 56.7 %all-gather.18.cloned.1.call-start = ((), (), s32[]{:S(2)}) async-start(), calls=%async_computation.10 | async-start | bytes 1572864 | tf_op jit(solution)/shard_map/all_gather | solution.py:137
  13.8 133.3 %all-gather.22.cloned.1.call-start = ((), (), s32[]{:S(2)}) async-start(), calls=%async_computation.12 | async-start | bytes 4718592 | tf_op jit(solution)/shard_map/all_gather | solution.py:165
  49.6 171.7 %all-gather.26.cloned.1.call-start = ((), (), s32[]{:S(2)}) async-start(), calls=%async_computation.14 | async-start | bytes 4718592 | tf_op jit(solution)/shard_map/all_gather | solution.py:166
  64.2 230.2 %all-gather.28.cloned.1.call-start = ((), (), s32[]{:S(2)}) async-start(), calls=%async_computation.15 | async-start | bytes 1572864 | tf_op jit(solution)/shard_map/all_gather | solution.py:142
  65.0 263.2 %reduce-scatter.8.cloned.1.call-start = ((), (), s32[]{:S(2)}) async-start(), calls=%async_computation.16 | async-start | bytes 3145728 | tf_op jit(solution)/shard_map/reduce_scatter | solution.py:153
  297.9 43.6 %all-gather.32.cloned.1.call-start = ((), (), s32[]{:S(2)}) async-start(), calls=%async_computation.18 | async-start | bytes 4325376 | tf_op jit(solution)/shard_map/all_gather | solution.py:140
  298.7 67.4 %all-gather.30.cloned.1.call-start = ((), (), s32[]{:S(2)}) async-start(), calls=%async_computation.17 | async-start | bytes 1572864 | tf_op jit(solution)/shard_map/all_gather | solution.py:150
  330.6 48.9 %all-gather.34.cloned.1.call-start = ((), (), s32[]{:S(2)}) async-start(), calls=%async_computation.19 | async-start | bytes 4325376 | tf_op jit(solution)/shard_map/all_gather | solution.py:141
  331.3 62.6 %all-gather.36.cloned.1.call-start = ((), (), s32[]{:S(2)}) async-start(), calls=%async_computation.20 | async-start | bytes 4325376 | tf_op jit(solution)/shard_map/all_gather | solution.py:143
  331.9 109.7 %reduce-scatter.10.cloned.1.call-start = ((), (), s32[]{:S(2)}) async-start(), calls=%async_computation.21 | async-start | bytes 3145728 | tf_op jit(solution)/shard_map/reduce_scatter | solution.py:153
  399.4 66.0 %all-gather.38.cloned.1.call-start = ((), (), s32[]{:S(2)}) async-start(), calls=%async_computation.22 | async-start | bytes 1572864 | tf_op jit(solution)/shard_map/all_gather | solution.py:150
  443.9 66.0 %reduce-scatter.12.cloned.1.call-start = ((), (), s32[]{:S(2)}) async-start(), calls=%async_computation.23 | async-start | bytes 3145728 | tf_op jit(solution)/shard_map/reduce_scatter | solution.py:153
  477.9 57.6 %all-gather.40.cloned.1.call-start = ((), (), s32[]{:S(2)}) async-start(), calls=%async_computation.24 | async-start | bytes 1572864 | tf_op jit(solution)/shard_map/all_gather | solution.py:150
  514.0 319.8 %reduce-scatter.14.cloned.1.call-start = ((), (), s32[]{:S(2)}) async-start(), calls=%async_computation.25 | async-start | bytes 4718592 | tf_op jit(solution)/shard_map/reduce_scatter | solution.py:201
  745.2 179.9 %reduce-scatter.16.cloned.1.call-start = ((), (), s32[]{:S(2)}) async-start(), calls=%async_computation.26 | async-start | bytes 4718592 | tf_op jit(solution)/shard_map/reduce_scatter | solution.py:204
  751.9 213.3 %reduce-scatter.20.cloned.1.call-start = ((), (), s32[]{:S(2)}) async-start(), calls=%async_computation.28 | async-start | bytes 19267584 | tf_op jit(solution)/shard_map/reduce_scatter | solution.py:225
  943.5 59.0 %reduce-scatter.18.cloned.1.call-start = ((), (), s32[]{:S(2)}) async-start(), calls=%async_computation.27 | async-start | bytes 3145728 | tf_op jit(solution)/shard_map/reduce_scatter | solution.py:153
  950.4 1027.1 %all-gather.42.cloned.1.call-start = ((), (), s32[]{:S(2)}) async-start(), calls=%async_computation.29 | async-start | bytes 57802752 | tf_op jit(solution)/shard_map/all_gather | solution.py:242
  966.1 161.2 %copy-start.23 = (f32[256]{0:T(256)S(1)}, f32[256]{0:T(256)}, u32[]{:S(2)}) copy-start(f32[256]{0:T(256)} %copy-done.22) | copy-start | bytes 3076
  966.1 161.2 %copy-start.6 = (f32[256,1024]{1,0:T(8,128)S(1)}, f32[256,1024]{1,0:T(8,128)}, u32[]{:S(2)}) copy-start(f32[256,1024]{1,0:T(8,128)} %get-tuple-element.277) | copy-start | bytes 3145732
  966.1 14.5 all-to-all-start.1
  (52 other events, 620.8 us)
Sparse Core Ops, SparseCore 0:
  11.8 23.9 all-gather.15
  37.4 9.0 all-gather.19
  48.0 10.1 all-gather.23
  59.7 10.1 all-gather.17
  72.5 74.5 all-gather.21
  149.6 71.6 all-gather.25
  222.8 7.2 all-gather.27
  298.1 30.0 reduce-scatter.7
  329.8 11.7 all-gather.31
  343.6 22.4 all-gather.29
  367.7 11.7 all-gather.33
  381.0 12.8 all-gather.35
  399.5 33.4 reduce-scatter.9
  444.0 21.2 all-gather.37
  478.0 31.8 reduce-scatter.11
  514.2 21.2 all-gather.39
  745.3 88.4 reduce-scatter.13
  837.3 87.7 reduce-scatter.15
  943.6 21.5 reduce-scatter.19
  967.9 34.5 reduce-scatter.17
  1004.0 973.4 all-gather.41
